TPU v7x, 32 devices: a whole 2x2x4 slice. The times are simulated.
32 devices in a mesh: section: 4 (over y, x), fsdp: 8 (over z, core).
Axes of the slice: x: 2, y: 2, z: 4, core: 2. Of those that a mesh axis runs over, the one named last changes fastest.
Arguments:
- master: float32 [4, 64, 4096], P('section', 'fsdp'), may hold values from -0.12 to 0.12
- first_moment: float32 [4, 64, 4096], P('section', 'fsdp'), may hold values from -0.2 to 0.2
- second_moment: float32 [4, 64, 4096], P('section', 'fsdp'), may hold values from 0.25 to 1
- gradient: float32 [4, 64, 4096], P('section', 'fsdp'), may hold values from -64 to 64
Outputs:
- new_master: float32 [4, 64, 4096], P('section', 'fsdp')
- new_first: float32 [4, 64, 4096], P('section', 'fsdp')
- new_second: float32 [4, 64, 4096], P('section', 'fsdp')
- weights: bfloat16 [4, 64, 4096], P('section')
- grad_rms: float32 [], replicated
All inputs are finite; a program needn't handle non-finite values.
Results may differ from a plain program's by a relative error of at most 0.001.
Values may be sent and summed in bfloat16 or wider, within the bound.
A program may use at most 64 MiB of HBM per device.

v0:
```python
import jax
import jax.numpy as jnp
from jax import lax
from jax.sharding import PartitionSpec as P

BETA_ONE = 0.9
BETA_TWO = 0.95
LEARN_RATE = 0.05
DECAY = 0.1
EPSILON = 1e-08
BIAS_STEPS = 10.0


def adamw_part(master, first_moment, second_moment, gradient, clip_scale):
    scaled = clip_scale * gradient
    new_first = BETA_ONE * first_moment + (1.0 - BETA_ONE) * scaled
    new_second = BETA_TWO * second_moment + (1.0 - BETA_TWO) * scaled * scaled
    first_hat = new_first / (1.0 - BETA_ONE**BIAS_STEPS)
    second_hat = new_second / (1.0 - BETA_TWO**BIAS_STEPS)
    update = first_hat / (jnp.sqrt(second_hat) + EPSILON)
    new_master = master * (1.0 - LEARN_RATE * DECAY) - LEARN_RATE * update
    return (new_master, new_first, new_second)


def local(master, first_moment, second_moment, gradient):
    partial_sq = jnp.sum(gradient * gradient)
    within = lax.psum(partial_sq, "fsdp")
    squares = lax.psum(within, "section")
    grad_norm = jnp.sqrt(squares)
    param_count = float(
        lax.axis_size("section")
        * lax.axis_size("fsdp")
        * gradient.shape[0]
        * gradient.shape[1]
        * gradient.shape[2]
    )
    limit = jnp.float32(0.5 * param_count**0.5)
    clip_scale = limit / jnp.maximum(grad_norm, limit)
    grad_rms = grad_norm / jnp.float32(param_count**0.5)
    new_master, new_first, new_second = adamw_part(
        master, first_moment, second_moment, gradient, clip_scale
    )
    weights = lax.all_gather(new_master.astype(jnp.bfloat16), "fsdp", axis=1, tiled=True)
    return (new_master, new_first, new_second, weights, grad_rms)


def solution(mesh):
    placed = (
        P("section", "fsdp", None),
        P("section", "fsdp", None),
        P("section", "fsdp", None),
        P("section", "fsdp", None),
    )
    return jax.shard_map(
        local,
        mesh=mesh,
        in_specs=placed,
        out_specs=(
            P("section", "fsdp", None),
            P("section", "fsdp", None),
            P("section", "fsdp", None),
            P("section", None, None),
            P(),
        ),
        check_vma=False,
    )
```

profile of v0, /device:TPU:0, one launch (start us, length us, event | category | flops | bytes accessed | tf_op | source)
XLA Modules:
  0.0 50.9 jit_solution(5301626764726928907)
XLA Ops:
  0.6 0.0 copy-start
  0.6 1.6 %multiply_reduce_fusion = f32[]{:T(128)} fusion(f32[1,8,4096]{2,1,0:T(8,128)} %param.7), kind=kLoop, calls=%fused_computation.4 | loop fusion | flops 65535 | bytes 131076 | tf_op jit(solution)/shard_map/reduce_sum | solution.py:26
  2.2 18.7 %psum.14 = f32[]{:T(128)} all-reduce(f32[]{:T(128)} %multiply_reduce_fusion), channel_id=1, replica_groups=mesh['section'=4,'fsdp'=8] {'fsdp'}, use_global_device_ids=true, to_apply=%region_1.0 | all-reduce | flops 1 | bytes 8 | tf_op jit(solution)/shard_map/psum | solution.py:27
  21.0 10.5 %psum.15 = f32[]{:T(128)} all-reduce(f32[]{:T(128)} %psum.14), channel_id=1, replica_groups=mesh['section'=4,'fsdp'=8] {'section'}, use_global_device_ids=true, to_apply=%region_2.0 | all-reduce | flops 1 | bytes 8 | tf_op jit(solution)/shard_map/psum | solution.py:28
  32.2 0.0 copy-done
  32.2 1.8 %fusion.1 = (bf16[1,8,4096]{2,1,0:T(8,128)(2,1)S(1)}, f32[1,8,4096]{2,1,0:T(8,128)}, f32[1,8,4096]{2,1,0:T(8,128)}, f32[1,8,4096]{2,1,0:T(8,128)}) fusion(f32[1,8,4096]{2,1,0:T(8,128)} %param.4, f32[1,8,4096]{2,1,0:T(8,128)S(1)} %copy-done, f32[]{:T(128)S(6)} %div.21, f32[1,8,4096]{2,1,0:T(8,128)} %param.5, f32[1,8,4096]{2,1,0:T(8,128)} %param.6), kind=kLoop, calls=%fused_computation.5 | loop fusion | flops 524288 | bytes 983044 | tf_op jit(solution)/shard_map/convert_element_type | solution.py:43
  34.1 14.9 %all_gather.3 = bf16[1,64,4096]{2,1,0:T(8,128)(2,1)S(1)} all-gather(bf16[1,8,4096]{2,1,0:T(8,128)(2,1)S(1)} %get-tuple-element.5), channel_id=1, replica_groups=mesh['section'=4,'fsdp'=8] {'fsdp'}, dimensions={1}, use_global_device_ids=true | all-gather | bytes 589824 | tf_op jit(solution)/shard_map/all_gather | solution.py:43
  49.0 0.8 %copy.10 = bf16[1,64,4096]{2,1,0:T(8,128)(2,1)} copy(bf16[1,64,4096]{2,1,0:T(8,128)(2,1)S(1)} %all_gather.3) | data formatting | bytes 1048576
Async XLA Ops:
  0.6 31.6 %copy-start = (f32[1,8,4096]{2,1,0:T(8,128)S(1)}, f32[1,8,4096]{2,1,0:T(8,128)}, u32[]{:S(2)}) copy-start(f32[1,8,4096]{2,1,0:T(8,128)} %param.7) | copy-start | bytes 393220
where the time goes:
time: 51.1 us; the launch traced here: 50.9 us
  blocking collectives  44.2 us (86%)
  other arithmetic  3.44 us (7%)
  between operations  2.51 us (5%)
  local copies, waits for them, and re-layouts  0.8 us (2%)
    psum x1, blocking collectives, local(): within = lax.psum(partial_sq, 'fsdp')  18.7 us
    all_gather x1, blocking collectives, local(): lax.all_gather(new_master.astype(jnp.bfloat16), 'fsdp', axis=1, tiled=True)  14.9 us
    psum x1, blocking collectives, local(): squares = lax.psum(within, 'section')  10.5 us
    convert_element_type x1, other arithmetic, local(): new_master.astype(jnp.bfloat16)  1.83 us
    reduce_sum x1, other arithmetic, local(): partial_sq = jnp.sum(gradient * gradient)  1.61 us

commit v1 on v0

v1 whole, which is shorter than its diff:
```python
import functools

import jax
import jax.numpy as jnp
from jax import lax
from jax.experimental import pallas as pl
from jax.experimental.pallas import tpu as pltpu
from jax.sharding import PartitionSpec as P

BETA_ONE = 0.9
BETA_TWO = 0.95
LEARN_RATE = 0.05
DECAY = 0.1
EPSILON = 1e-08
BIAS_STEPS = 10.0
MESH = pl.DeviceIdType.MESH
UNROLL_MOST = 128


def for_each(count, body):
    if count <= UNROLL_MOST:
        for i in range(count):
            body(i)
    else:
        lax.fori_loop(0, count, lambda i, carry: (body(i), carry)[1], 0)


def step_kernel(
    sections, shards, params,
    master_hbm, first_hbm, second_hbm, grad_hbm,
    new_master, new_first, new_second, weights, rms,
    master, first, second, grad, part, parts,
    load_sem, part_send, part_recv, block_send, block_recv, pair_send,
):
    my_section = lax.axis_index("section")
    my_shard = lax.axis_index("fsdp")
    total = sections * shards
    me = my_section * shards + my_shard

    loads = [
        pltpu.make_async_copy(src.at[0], dst, load_sem.at[i])
        for i, (src, dst) in enumerate(
            ((grad_hbm, grad), (master_hbm, master), (first_hbm, first), (second_hbm, second))
        )
    ]
    for load in loads:
        load.start()

    def peer(i):
        s = lax.rem(my_section + i // shards, sections)
        f = lax.rem(my_shard + i % shards, shards)
        return s, f

    barrier = pltpu.get_barrier_semaphore()

    def greet(i):
        pl.semaphore_signal(barrier, inc=1, device_id=peer(i + 1), device_id_type=MESH)

    for_each(total - 1, greet)

    loads[0].wait()
    g = grad[...]
    squares = g * g
    width = squares.shape[1]
    folded = squares[:, :128]
    for j in range(1, width // 128):
        folded += squares[:, j * 128 : (j + 1) * 128]
    row = jnp.sum(folded, axis=0, keepdims=True)
    part[...] = row
    parts[pl.ds(me, 1), :] = row

    pl.semaphore_wait(barrier, total - 1)

    def send_part(i):
        s, f = peer(i + 1)
        pltpu.make_async_remote_copy(
            src_ref=part,
            dst_ref=parts.at[pl.ds(me, 1)],
            send_sem=part_send,
            recv_sem=part_recv,
            device_id=(s, f),
            device_id_type=MESH,
        ).start()

    for_each(total - 1, send_part)
    for load in loads[1:]:
        load.wait()
    others = parts.at[pl.ds(0, total - 1)]
    pltpu.make_async_copy(others, others, part_recv).wait()

    squares_all = jnp.sum(jnp.sum(parts[...], axis=0, keepdims=True), axis=1, keepdims=True)
    norm = jnp.sqrt(squares_all)
    limit = jnp.float32(0.5 * params**0.5)
    clip = limit / jnp.maximum(norm, limit)
    rms[...] = norm / jnp.float32(params**0.5)

    scaled = clip * g
    nf = BETA_ONE * first[...] + (1.0 - BETA_ONE) * scaled
    ns = BETA_TWO * second[...] + (1.0 - BETA_TWO) * scaled * scaled
    first_hat = nf / (1.0 - BETA_ONE**BIAS_STEPS)
    second_hat = ns / (1.0 - BETA_TWO**BIAS_STEPS)
    update = first_hat / (jnp.sqrt(second_hat) + EPSILON)
    nm = master[...] * (1.0 - LEARN_RATE * DECAY) - LEARN_RATE * update
    weights[my_shard] = nm.astype(jnp.bfloat16)
    new_master[0] = nm
    new_first[0] = nf
    new_second[0] = ns

    cores = 2 if shards % 2 == 0 else 1
    chips = shards // cores
    core = my_shard % cores
    chip = my_shard // cores
    partner = chip * cores + (cores - 1 - core)

    def to(block, shard, send_sem):
        return pltpu.make_async_remote_copy(
            src_ref=weights.at[block],
            dst_ref=weights.at[block],
            send_sem=send_sem,
            recv_sem=block_recv.at[block],
            device_id=(my_section, shard),
            device_id_type=MESH,
        )

    def across(i):
        other = lax.rem(chip + i + 1, chips) * cores + core
        to(my_shard, other, block_send.at[i]).start()

    for_each(chips - 1, across)
    if cores == 2:
        to(my_shard, partner, pair_send.at[chips - 1]).start()

    def arrived(i):
        block = lax.rem(chip + chips - i - 1, chips) * cores + core
        to(block, partner, block_send.at[i]).wait_recv()
        if cores == 2:
            to(block, partner, pair_send.at[i]).start()

    for_each(chips - 1, arrived)
    if cores == 2:

        def arrived_pair(i):
            block = lax.rem(chip + chips - i - 1, chips) * cores + (1 - core)
            to(block, partner, pair_send.at[i]).wait_recv()

        for_each(chips, arrived_pair)

        def sent_pair(i):
            to(my_shard, partner, pair_send.at[i]).wait_send()

        for_each(chips, sent_pair)

    def sent(i):
        to(my_shard, partner, block_send.at[i]).wait_send()

    for_each(chips - 1, sent)
    pltpu.make_async_copy(others, others, part_send).wait()


def local(sections, shards, master, first_moment, second_moment, gradient):
    _, rows, width = gradient.shape
    params = float(sections * shards * rows * width)
    total = sections * shards
    chips = max(shards // 2, 1) if shards % 2 == 0 else shards
    vmem = pl.BlockSpec(memory_space=pltpu.VMEM)
    hbm = pl.BlockSpec(memory_space=pl.ANY)
    block = jax.ShapeDtypeStruct((1, rows, width), jnp.float32)
    new_master, new_first, new_second, weights, rms = pl.pallas_call(
        functools.partial(step_kernel, sections, shards, params),
        out_shape=(
            block,
            block,
            block,
            jax.ShapeDtypeStruct((shards, rows, width), jnp.bfloat16),
            jax.ShapeDtypeStruct((1, 1), jnp.float32),
        ),
        in_specs=[hbm] * 4,
        out_specs=(vmem,) * 5,
        scratch_shapes=[pltpu.VMEM((rows, width), jnp.float32)] * 4
        + [
            pltpu.VMEM((1, 128), jnp.float32),
            pltpu.VMEM((total, 128), jnp.float32),
            pltpu.SemaphoreType.DMA((4,)),
            pltpu.SemaphoreType.DMA,
            pltpu.SemaphoreType.DMA,
            pltpu.SemaphoreType.DMA((chips,)),
            pltpu.SemaphoreType.DMA((shards,)),
            pltpu.SemaphoreType.DMA((chips,)),
        ],
        compiler_params=pltpu.CompilerParams(collective_id=0, has_side_effects=True),
    )(master, first_moment, second_moment, gradient)
    return (
        new_master,
        new_first,
        new_second,
        weights.reshape(1, shards * rows, width),
        rms.reshape(()),
    )


def solution(mesh):
    placed = (P("section", "fsdp", None),) * 4
    return jax.shard_map(
        functools.partial(local, mesh.shape["section"], mesh.shape["fsdp"]),
        mesh=mesh,
        in_specs=placed,
        out_specs=(
            P("section", "fsdp", None),
            P("section", "fsdp", None),
            P("section", "fsdp", None),
            P("section", None, None),
            P(),
        ),
        check_vma=False,
    )
```

time: 51.1 us -> 27.9 us (0.55)
  blocking collectives: 44.2 us -> 0 us
  Pallas kernels: 0 us -> 19.7 us
  local copies, waits for them, and re-layouts: 0.8 us -> 5.56 us
  other arithmetic: 3.44 us -> 0 us
    psum x2 -> x0, blocking collectives: 29.2 us -> none  [the longest x1 18.7 us: local(): within = lax.psum(partial_sq, 'fsdp')]
    pallas_call x0 -> x1, Pallas kernels: none -> 19.7 us  [local(): pl.pallas_call(functools.partial(step_kernel, sections, shards, params),...]
    all_gather x1 -> x0, blocking collectives: 14.9 us -> none  [local(): lax.all_gather(new_master.astype(jnp.bfloat16), 'fsdp', axis=1, tiled=True)]
    unnamed x3 -> x6, local copies, waits for them, and re-layouts: 0.8 us -> 5.56 us
    convert_element_type x1 -> x0, other arithmetic: 1.83 us -> none  [local(): new_master.astype(jnp.bfloat16)]
    reduce_sum x1 -> x0, other arithmetic: 1.61 us -> none  [local(): partial_sq = jnp.sum(gradient * gradient)]
where the time goes in v1:
time: 27.9 us; the launch traced here: 27.7 us
  Pallas kernels  19.7 us (71%)
  local copies, waits for them, and re-layouts  5.56 us (20%)
  between operations  2.4 us (9%)
    pallas_call x1, Pallas kernels, local(): pl.pallas_call(functools.partial(step_kernel, sections, shards, params),...  19.7 us
    unnamed x6, local copies, waits for them, and re-layouts  5.56 us

profile of v1, /device:TPU:0, one launch (start us, length us, event | category | flops | bytes accessed | tf_op | source)
XLA Modules:
  0.0 27.7 jit_solution(11037632305110441317)
XLA Ops:
  0.6 19.7 %shard_map.83 = (f32[1,8,4096]{2,1,0:T(8,128)}, f32[1,8,4096]{2,1,0:T(8,128)}, f32[1,8,4096]{2,1,0:T(8,128)}, bf16[8,8,4096]{2,1,0:T(8,128)(2,1)}, f32[1,1]{1,0:T(1,128)}) custom-call(f32[1,8,4096]{2,1,0:T(8,128)} %master_hbm.1, f32[1,8,4096]{2,1,0:T(8,128)} %first_hbm.1, f32[1,8,4096]{2,1,0:T(8,128)} %second_hbm.1, f32[1,8,4096]{2,1,0:T(8,128)} %grad_hbm.1), custom_call_target="tpu_custom_call" | custom-call | tf_op jit(solution)/shard_map/pallas_call | solution.py:168
  20.4 0.0 copy-start
  20.4 1.6 %copy.14 = f32[1,8,4096]{2,1,0:T(8,128)} copy(f32[1,8,4096]{2,1,0:T(8,128)} %get-tuple-element.20) | data formatting | bytes 262144
  22.0 1.6 %copy.15 = f32[1,8,4096]{2,1,0:T(8,128)} copy(f32[1,8,4096]{2,1,0:T(8,128)} %get-tuple-element.21) | data formatting | bytes 262144
  23.6 1.6 %copy.16 = f32[1,8,4096]{2,1,0:T(8,128)} copy(f32[1,8,4096]{2,1,0:T(8,128)} %get-tuple-element.22) | data formatting | bytes 262144
  25.1 0.0 copy-done
  25.1 0.8 %copy.17 = bf16[1,64,4096]{2,1,0:T(8,128)(2,1)} copy(bf16[1,64,4096]{2,1,0:T(8,128)(2,1)S(1)} %bitcast.2) | data formatting | bytes 1048576
Async XLA Ops:
  20.4 4.8 %copy-start = (bf16[8,8,4096]{2,1,0:T(8,128)(2,1)S(1)}, bf16[8,8,4096]{2,1,0:T(8,128)(2,1)}, u32[]{:S(2)}) copy-start(bf16[8,8,4096]{2,1,0:T(8,128)(2,1)} %get-tuple-element.13) | copy-start | bytes 1572868

commit v2 on v1

--- a/solution.py
+++ b/solution.py
@@ -15,6 +15,7 @@
 BIAS_STEPS = 10.0
 MESH = pl.DeviceIdType.MESH
 UNROLL_MOST = 128
+VMEM_GRANT = 16 * 1024 * 1024
 
 
 def for_each(count, body):
@@ -157,6 +158,17 @@
     pltpu.make_async_copy(others, others, part_send).wait()
 
 
+def store_kernel(*refs):
+    count = len(refs) // 2
+    copies = [
+        pltpu.make_async_copy(refs[i], refs[count + i], refs[-1].at[i]) for i in range(count)
+    ]
+    for copy in copies:
+        copy.start()
+    for copy in copies:
+        copy.wait()
+
+
 def local(sections, shards, master, first_moment, second_moment, gradient):
     _, rows, width = gradient.shape
     params = float(sections * shards * rows * width)
@@ -164,16 +176,11 @@
     chips = max(shards // 2, 1) if shards % 2 == 0 else shards
     vmem = pl.BlockSpec(memory_space=pltpu.VMEM)
     hbm = pl.BlockSpec(memory_space=pl.ANY)
-    block = jax.ShapeDtypeStruct((1, rows, width), jnp.float32)
-    new_master, new_first, new_second, weights, rms = pl.pallas_call(
+    results = [((1, rows, width), jnp.float32)] * 3
+    results += [((shards, rows, width), jnp.bfloat16), ((1, 1), jnp.float32)]
+    held = pl.pallas_call(
         functools.partial(step_kernel, sections, shards, params),
-        out_shape=(
-            block,
-            block,
-            block,
-            jax.ShapeDtypeStruct((shards, rows, width), jnp.bfloat16),
-            jax.ShapeDtypeStruct((1, 1), jnp.float32),
-        ),
+        out_shape=tuple(pltpu.VMEM(shape, dtype) for shape, dtype in results),
         in_specs=[hbm] * 4,
         out_specs=(vmem,) * 5,
         scratch_shapes=[pltpu.VMEM((rows, width), jnp.float32)] * 4
@@ -187,8 +194,18 @@
             pltpu.SemaphoreType.DMA((shards,)),
             pltpu.SemaphoreType.DMA((chips,)),
         ],
-        compiler_params=pltpu.CompilerParams(collective_id=0, has_side_effects=True),
+        compiler_params=pltpu.CompilerParams(
+            collective_id=0, has_side_effects=True, vmem_limit_bytes=VMEM_GRANT
+        ),
     )(master, first_moment, second_moment, gradient)
+    new_master, new_first, new_second, weights, rms = pl.pallas_call(
+        store_kernel,
+        out_shape=tuple(jax.ShapeDtypeStruct(shape, dtype) for shape, dtype in results),
+        in_specs=[vmem] * 5,
+        out_specs=(hbm,) * 5,
+        scratch_shapes=[pltpu.SemaphoreType.DMA((5,))],
+        compiler_params=pltpu.CompilerParams(vmem_limit_bytes=VMEM_GRANT),
+    )(*[pltpu.with_memory_space_constraint(x, pltpu.VMEM) for x in held])
     return (
         new_master,
         new_first,

time: 27.9 us -> 25.9 us (0.928)
  local copies, waits for them, and re-layouts: 5.56 us -> 3.61 us
  between operations: 2.4 us -> 0.65 us
  Pallas kernels: 19.7 us -> 21.4 us
    unnamed x6 -> x8, local copies, waits for them, and re-layouts: 5.56 us -> 3.61 us
    pallas_call x0 -> x1, Pallas kernels: none -> 1.52 us  [local(): pl.pallas_call(store_kernel, out_shape=tuple((jax.ShapeDtypeStruct(shape,...]
where the time goes in v2:
time: 25.9 us; the launch traced here: 25.7 us
  Pallas kernels  21.4 us (83%)
  local copies, waits for them, and re-layouts  3.61 us (14%)
  between operations  0.65 us (3%)
    pallas_call x1, Pallas kernels, local(): pl.pallas_call(functools.partial(step_kernel, sections, shards, params),...  19.9 us
    unnamed x8, local copies, waits for them, and re-layouts  3.61 us
    pallas_call x1, Pallas kernels, local(): pl.pallas_call(store_kernel, out_shape=tuple((jax.ShapeDtypeStruct(shape,...  1.52 us

profile of v2, /device:TPU:0, one launch (start us, length us, event | category | flops | bytes accessed | tf_op | source)
XLA Modules:
  0.0 25.7 jit_solution(5932206543392940003)
XLA Ops:
  0.6 0.0 copy-start
  0.6 0.9 %copy-done = f32[1,8,4096]{2,1,0:T(8,128)S(1)} copy-done((f32[1,8,4096]{2,1,0:T(8,128)S(1)}, f32[1,8,4096]{2,1,0:T(8,128)}, u32[]{:S(2)}) %copy-start) | copy-done | bytes 131096
  1.5 0.0 copy-start.1
  1.5 0.9 %copy-done.1 = f32[1,8,4096]{2,1,0:T(8,128)S(1)} copy-done((f32[1,8,4096]{2,1,0:T(8,128)S(1)}, f32[1,8,4096]{2,1,0:T(8,128)}, u32[]{:S(2)}) %copy-start.1) | copy-done | bytes 131096
  2.4 0.0 copy-start.2
  2.4 0.9 %copy-done.2 = f32[1,8,4096]{2,1,0:T(8,128)S(1)} copy-done((f32[1,8,4096]{2,1,0:T(8,128)S(1)}, f32[1,8,4096]{2,1,0:T(8,128)}, u32[]{:S(2)}) %copy-start.2) | copy-done | bytes 131096
  3.3 0.0 copy-start.3
  3.3 0.9 %copy-done.3 = f32[1,8,4096]{2,1,0:T(8,128)S(1)} copy-done((f32[1,8,4096]{2,1,0:T(8,128)S(1)}, f32[1,8,4096]{2,1,0:T(8,128)}, u32[]{:S(2)}) %copy-start.3) | copy-done | bytes 131096
  4.3 19.9 %shard_map.83 = (f32[1,8,4096]{2,1,0:T(8,128)S(1)}, f32[1,8,4096]{2,1,0:T(8,128)S(1)}, f32[1,8,4096]{2,1,0:T(8,128)S(1)}, bf16[8,8,4096]{2,1,0:T(8,128)(2,1)S(1)}, f32[1,1]{1,0:T(1,128)}) custom-call(f32[1,8,4096]{2,1,0:T(8,128)S(1)} %copy-done, f32[1,8,4096]{2,1,0:T(8,128)S(1)} %copy-done.1, f32[1,8,4096]{2,1,0:T(8,128)S(1)} %copy-done.2, ...), custom_call_target="tpu_custom_call" | custom-call | tf_op jit(solution)/shard_map/pallas_call | solution.py:181
  24.2 1.5 %shard_map.84 = (f32[1,8,4096]{2,1,0:T(8,128)}, f32[1,8,4096]{2,1,0:T(8,128)}, f32[1,8,4096]{2,1,0:T(8,128)}, bf16[8,8,4096]{2,1,0:T(8,128)(2,1)}, f32[1,1]{1,0:T(1,128)}) custom-call(f32[1,8,4096]{2,1,0:T(8,128)S(1)} %get-tuple-element.15.refs_0_, f32[1,8,4096]{2,1,0:T(8,128)S(1)} %get-tuple-element.16.refs_1_, ...), custom_call_target="tpu_custom_call" | custom-call | tf_op jit(solution)/shard_map/pallas_call | solution.py:201
Async XLA Ops:
  0.6 0.9 %copy-start = (f32[1,8,4096]{2,1,0:T(8,128)S(1)}, f32[1,8,4096]{2,1,0:T(8,128)}, u32[]{:S(2)}) copy-start(f32[1,8,4096]{2,1,0:T(8,128)} %master_hbm.1) | copy-start | bytes 393220
  1.5 0.9 %copy-start.1 = (f32[1,8,4096]{2,1,0:T(8,128)S(1)}, f32[1,8,4096]{2,1,0:T(8,128)}, u32[]{:S(2)}) copy-start(f32[1,8,4096]{2,1,0:T(8,128)} %first_hbm.1) | copy-start | bytes 393220
  2.4 0.9 %copy-start.2 = (f32[1,8,4096]{2,1,0:T(8,128)S(1)}, f32[1,8,4096]{2,1,0:T(8,128)}, u32[]{:S(2)}) copy-start(f32[1,8,4096]{2,1,0:T(8,128)} %second_hbm.1) | copy-start | bytes 393220
  3.3 0.9 %copy-start.3 = (f32[1,8,4096]{2,1,0:T(8,128)S(1)}, f32[1,8,4096]{2,1,0:T(8,128)}, u32[]{:S(2)}) copy-start(f32[1,8,4096]{2,1,0:T(8,128)} %grad_hbm.1) | copy-start | bytes 393220

commit v3 on v2

--- a/solution.py
+++ b/solution.py
@@ -1,4 +1,5 @@
 import functools
+import math
 
 import jax
 import jax.numpy as jnp
@@ -14,8 +15,10 @@
 EPSILON = 1e-08
 BIAS_STEPS = 10.0
 MESH = pl.DeviceIdType.MESH
-UNROLL_MOST = 128
-VMEM_GRANT = 16 * 1024 * 1024
+UNROLL_MOST = 40
+PIECES = 1
+VMEM_MOST = 67043328
+GRANT_MOST = 60 * 1024 * 1024
 
 
 def for_each(count, body):
@@ -27,11 +30,11 @@
 
 
 def step_kernel(
-    sections, shards, params,
+    sections, shards, params, pieces,
     master_hbm, first_hbm, second_hbm, grad_hbm,
     new_master, new_first, new_second, weights, rms,
     master, first, second, grad, part, parts,
-    load_sem, part_send, part_recv, block_send, block_recv, pair_send,
+    load_sem, part_send, part_recv, line_send, line_recv, pair_send, pair_recv,
 ):
     my_section = lax.axis_index("section")
     my_shard = lax.axis_index("fsdp")
@@ -44,8 +47,7 @@
             ((grad_hbm, grad), (master_hbm, master), (first_hbm, first), (second_hbm, second))
         )
     ]
-    for load in loads:
-        load.start()
+    loads[0].start()
 
     def peer(i):
         s = lax.rem(my_section + i // shards, sections)
@@ -58,6 +60,9 @@
         pl.semaphore_signal(barrier, inc=1, device_id=peer(i + 1), device_id_type=MESH)
 
     for_each(total - 1, greet)
+
+    for load in loads[1:]:
+        load.start()
 
     loads[0].wait()
     g = grad[...]
@@ -111,50 +116,79 @@
     chips = shards // cores
     core = my_shard % cores
     chip = my_shard // cores
-    partner = chip * cores + (cores - 1 - core)
-
-    def to(block, shard, send_sem):
+    pair = 1 - core
+    cut = width // pieces
+
+    def copy(block, piece, shard, send_sem, recv_sem):
+        there = weights.at[block, :, pl.ds(piece * cut, cut)]
         return pltpu.make_async_remote_copy(
-            src_ref=weights.at[block],
-            dst_ref=weights.at[block],
+            src_ref=there,
+            dst_ref=there,
             send_sem=send_sem,
-            recv_sem=block_recv.at[block],
+            recv_sem=recv_sem,
             device_id=(my_section, shard),
             device_id_type=MESH,
         )
 
-    def across(i):
-        other = lax.rem(chip + i + 1, chips) * cores + core
-        to(my_shard, other, block_send.at[i]).start()
-
-    for_each(chips - 1, across)
-    if cores == 2:
-        to(my_shard, partner, pair_send.at[chips - 1]).start()
-
-    def arrived(i):
-        block = lax.rem(chip + chips - i - 1, chips) * cores + core
-        to(block, partner, block_send.at[i]).wait_recv()
+    def along(block_chip, piece, target):
+        block = block_chip * cores + core
+        return copy(
+            block, piece, target * cores + core, line_send.at[target], line_recv.at[block_chip, piece]
+        )
+
+    def over(block_chip, lane, piece):
+        block = block_chip * cores + lane
+        return copy(block, piece, chip * cores + pair, pair_send.at[block_chip], pair_recv.at[block_chip])
+
+    def hand(block_chip, piece):
         if cores == 2:
-            to(block, partner, pair_send.at[i]).start()
-
-    for_each(chips - 1, arrived)
-    if cores == 2:
-
-        def arrived_pair(i):
-            block = lax.rem(chip + chips - i - 1, chips) * cores + (1 - core)
-            to(block, partner, pair_send.at[i]).wait_recv()
-
-        for_each(chips, arrived_pair)
-
-        def sent_pair(i):
-            to(my_shard, partner, pair_send.at[i]).wait_send()
-
-        for_each(chips, sent_pair)
-
-    def sent(i):
-        to(my_shard, partner, block_send.at[i]).wait_send()
-
-    for_each(chips - 1, sent)
+            over(block_chip, core, piece).start()
+
+    def send(i):
+        far = chips - 1 - i
+        for piece in range(pieces):
+
+            @pl.when(chip + far < chips)
+            def _():
+                along(chip, piece, chip + far).start()
+
+            @pl.when(chip - far >= 0)
+            def _():
+                along(chip, piece, chip - far).start()
+
+    for_each(chips - 1, send)
+    for piece in range(pieces):
+        hand(chip, piece)
+
+    def receive(i):
+        for piece in range(pieces):
+
+            @pl.when(chip - i - 1 >= 0)
+            def _():
+                along(chip - i - 1, piece, chip).wait_recv()
+                hand(chip - i - 1, piece)
+
+            @pl.when(chip + i + 1 < chips)
+            def _():
+                along(chip + i + 1, piece, chip).wait_recv()
+                hand(chip + i + 1, piece)
+
+    for_each(chips - 1, receive)
+
+    def whole(block, sem):
+        ref = weights.at[block]
+        return pltpu.make_async_copy(ref, ref, sem)
+
+    def finish(i):
+        if cores == 2:
+            whole(i * cores + pair, pair_recv.at[i]).wait()
+            whole(i * cores + core, pair_send.at[i]).wait()
+
+        @pl.when(i != chip)
+        def _():
+            whole(my_shard, line_send.at[i]).wait()
+
+    for_each(chips, finish)
     pltpu.make_async_copy(others, others, part_send).wait()
 
 
@@ -173,13 +207,16 @@
     _, rows, width = gradient.shape
     params = float(sections * shards * rows * width)
     total = sections * shards
-    chips = max(shards // 2, 1) if shards % 2 == 0 else shards
+    chips = shards // 2 if shards % 2 == 0 else shards
+    pieces = PIECES if width % (PIECES * 128) == 0 else 1
     vmem = pl.BlockSpec(memory_space=pltpu.VMEM)
-    hbm = pl.BlockSpec(memory_space=pl.ANY)
+    hbm = pl.BlockSpec(memory_space=pltpu.HBM)
     results = [((1, rows, width), jnp.float32)] * 3
     results += [((shards, rows, width), jnp.bfloat16), ((1, 1), jnp.float32)]
+    room = sum(math.prod(shape) * jnp.dtype(dtype).itemsize for shape, dtype in results)
+    grant = min(GRANT_MOST, VMEM_MOST - room - rows * width * 2)
     held = pl.pallas_call(
-        functools.partial(step_kernel, sections, shards, params),
+        functools.partial(step_kernel, sections, shards, params, pieces),
         out_shape=tuple(pltpu.VMEM(shape, dtype) for shape, dtype in results),
         in_specs=[hbm] * 4,
         out_specs=(vmem,) * 5,
@@ -191,11 +228,12 @@
             pltpu.SemaphoreType.DMA,
             pltpu.SemaphoreType.DMA,
             pltpu.SemaphoreType.DMA((chips,)),
-            pltpu.SemaphoreType.DMA((shards,)),
+            pltpu.SemaphoreType.DMA((chips, pieces)),
+            pltpu.SemaphoreType.DMA((chips,)),
             pltpu.SemaphoreType.DMA((chips,)),
         ],
         compiler_params=pltpu.CompilerParams(
-            collective_id=0, has_side_effects=True, vmem_limit_bytes=VMEM_GRANT
+            collective_id=0, has_side_effects=True, vmem_limit_bytes=grant
         ),
     )(master, first_moment, second_moment, gradient)
     new_master, new_first, new_second, weights, rms = pl.pallas_call(
@@ -204,7 +242,7 @@
         in_specs=[vmem] * 5,
         out_specs=(hbm,) * 5,
         scratch_shapes=[pltpu.SemaphoreType.DMA((5,))],
-        compiler_params=pltpu.CompilerParams(vmem_limit_bytes=VMEM_GRANT),
+        compiler_params=pltpu.CompilerParams(vmem_limit_bytes=grant),
     )(*[pltpu.with_memory_space_constraint(x, pltpu.VMEM) for x in held])
     return (
         new_master,

time: 25.9 us -> 21.7 us (0.84)
  local copies, waits for them, and re-layouts: 3.61 us -> 0 us
  Pallas kernels: 21.4 us -> 20.9 us
    unnamed x8 -> x0, local copies, waits for them, and re-layouts: 3.61 us -> none
    pallas_call x1, Pallas kernels: 19.9 us -> 19.3 us  [local(): pl.pallas_call(functools.partial(step_kernel, sections, shards, params, p...]
where the time goes in v3:
time: 21.7 us; the launch traced here: 21.6 us
  Pallas kernels  20.9 us (96%)
  between operations  0.64 us (3%)
    pallas_call x1, Pallas kernels, local(): pl.pallas_call(functools.partial(step_kernel, sections, shards, params, p...  19.3 us
    pallas_call x1, Pallas kernels, local(): pl.pallas_call(store_kernel, out_shape=tuple((jax.ShapeDtypeStruct(shape,...  1.6 us

profile of v3, /device:TPU:0, one launch (start us, length us, event | category | flops | bytes accessed | tf_op | source)
XLA Modules:
  0.0 21.6 jit_solution(17811181081618264252)
XLA Ops:
  0.6 19.3 %shard_map.83 = (f32[1,8,4096]{2,1,0:T(8,128)S(1)}, f32[1,8,4096]{2,1,0:T(8,128)S(1)}, f32[1,8,4096]{2,1,0:T(8,128)S(1)}, bf16[8,8,4096]{2,1,0:T(8,128)(2,1)S(1)}, f32[1,1]{1,0:T(1,128)}) custom-call(f32[1,8,4096]{2,1,0:T(8,128)} %master_hbm.1, f32[1,8,4096]{2,1,0:T(8,128)} %first_hbm.1, f32[1,8,4096]{2,1,0:T(8,128)} %second_hbm.1, f32[1,8,4096]{2,1,0:T(8,128)} %grad_hbm.1), custom_call_target="tpu_custom_call" | custom-call | tf_op jit(solution)/shard_map/pallas_call | solution.py:218
  20.0 1.6 %shard_map.84 = (f32[1,8,4096]{2,1,0:T(8,128)}, f32[1,8,4096]{2,1,0:T(8,128)}, f32[1,8,4096]{2,1,0:T(8,128)}, bf16[8,8,4096]{2,1,0:T(8,128)(2,1)}, f32[1,1]{1,0:T(1,128)}) custom-call(f32[1,8,4096]{2,1,0:T(8,128)S(1)} %get-tuple-element.15.refs_0_, f32[1,8,4096]{2,1,0:T(8,128)S(1)} %get-tuple-element.16.refs_1_, ...), custom_call_target="tpu_custom_call" | custom-call | tf_op jit(solution)/shard_map/pallas_call | solution.py:239

commit v4 on v3

--- a/solution.py
+++ b/solution.py
@@ -98,7 +98,7 @@
     norm = jnp.sqrt(squares_all)
     limit = jnp.float32(0.5 * params**0.5)
     clip = limit / jnp.maximum(norm, limit)
-    rms[...] = norm / jnp.float32(params**0.5)
+    rms[...] = jnp.broadcast_to(norm / jnp.float32(params**0.5), rms.shape)
 
     scaled = clip * g
     nf = BETA_ONE * first[...] + (1.0 - BETA_ONE) * scaled
@@ -193,12 +193,13 @@
 
 
 def store_kernel(*refs):
-    count = len(refs) // 2
-    copies = [
-        pltpu.make_async_copy(refs[i], refs[count + i], refs[-1].at[i]) for i in range(count)
-    ]
-    for copy in copies:
+    held, outs, (rms, sem) = refs[:5], refs[5:10], refs[10:]
+    copies = [pltpu.make_async_copy(held[i], outs[i], sem.at[i]) for i in range(4)]
+    copies.append(pltpu.make_async_copy(rms, outs[4], sem.at[4]))
+    for copy in copies[:4]:
         copy.start()
+    rms[...] = held[4][:1, :1]
+    copies[4].start()
     for copy in copies:
         copy.wait()
 
@@ -212,7 +213,7 @@
     vmem = pl.BlockSpec(memory_space=pltpu.VMEM)
     hbm = pl.BlockSpec(memory_space=pltpu.HBM)
     results = [((1, rows, width), jnp.float32)] * 3
-    results += [((shards, rows, width), jnp.bfloat16), ((1, 1), jnp.float32)]
+    results += [((shards, rows, width), jnp.bfloat16), ((8, 128), jnp.float32)]
     room = sum(math.prod(shape) * jnp.dtype(dtype).itemsize for shape, dtype in results)
     grant = min(GRANT_MOST, VMEM_MOST - room - rows * width * 2)
     held = pl.pallas_call(
@@ -238,10 +239,11 @@
     )(master, first_moment, second_moment, gradient)
     new_master, new_first, new_second, weights, rms = pl.pallas_call(
         store_kernel,
-        out_shape=tuple(jax.ShapeDtypeStruct(shape, dtype) for shape, dtype in results),
+        out_shape=tuple(jax.ShapeDtypeStruct(shape, dtype) for shape, dtype in results[:4])
+        + (jax.ShapeDtypeStruct((1, 1), jnp.float32),),
         in_specs=[vmem] * 5,
         out_specs=(hbm,) * 5,
-        scratch_shapes=[pltpu.SemaphoreType.DMA((5,))],
+        scratch_shapes=[pltpu.VMEM((1, 1), jnp.float32), pltpu.SemaphoreType.DMA((5,))],
         compiler_params=pltpu.CompilerParams(vmem_limit_bytes=grant),
     )(*[pltpu.with_memory_space_constraint(x, pltpu.VMEM) for x in held])
     return (

time: 21.7 us -> 20.6 us (0.949)
  Pallas kernels: 20.9 us -> 19.8 us
    pallas_call x1, Pallas kernels: 1.6 us -> 0.97 us  [local(): pl.pallas_call(store_kernel, out_shape=tuple((jax.ShapeDtypeStruct(shape,...]
    pallas_call x1, Pallas kernels: 19.3 us -> 18.8 us  [local(): pl.pallas_call(functools.partial(step_kernel, sections, shards, params, p...]
where the time goes in v4:
time: 20.6 us; the launch traced here: 20.4 us
  Pallas kernels  19.8 us (96%)
  between operations  0.64 us (3%)
    pallas_call x1, Pallas kernels, local(): pl.pallas_call(functools.partial(step_kernel, sections, shards, params, p...  18.8 us
    pallas_call x1, Pallas kernels, local(): pl.pallas_call(store_kernel, out_shape=tuple((jax.ShapeDtypeStruct(shape,...  0.97 us

profile of v4, /device:TPU:0, one launch (start us, length us, event | category | flops | bytes accessed | tf_op | source)
XLA Modules:
  0.0 20.4 jit_solution(999992809055703258)
XLA Ops:
  0.6 18.8 %shard_map.83 = (f32[1,8,4096]{2,1,0:T(8,128)S(1)}, f32[1,8,4096]{2,1,0:T(8,128)S(1)}, f32[1,8,4096]{2,1,0:T(8,128)S(1)}, bf16[8,8,4096]{2,1,0:T(8,128)(2,1)S(1)}, f32[8,128]{1,0:T(8,128)S(1)}) custom-call(f32[1,8,4096]{2,1,0:T(8,128)} %master_hbm.1, f32[1,8,4096]{2,1,0:T(8,128)} %first_hbm.1, f32[1,8,4096]{2,1,0:T(8,128)} %second_hbm.1, f32[1,8,4096]{2,1,0:T(8,128)} %grad_hbm.1), custom_call_target="tpu_custom_call" | custom-call | tf_op jit(solution)/shard_map/pallas_call | solution.py:219
  19.4 1.0 %shard_map.84 = (f32[1,8,4096]{2,1,0:T(8,128)}, f32[1,8,4096]{2,1,0:T(8,128)}, f32[1,8,4096]{2,1,0:T(8,128)}, bf16[8,8,4096]{2,1,0:T(8,128)(2,1)}, f32[1,1]{1,0:T(1,128)}) custom-call(f32[1,8,4096]{2,1,0:T(8,128)S(1)} %get-tuple-element.15.refs_0_, f32[1,8,4096]{2,1,0:T(8,128)S(1)} %get-tuple-element.16.refs_1_, ...), custom_call_target="tpu_custom_call" | custom-call | tf_op jit(solution)/shard_map/pallas_call | solution.py:240

commit v5 on v4

--- a/solution.py
+++ b/solution.py
@@ -34,7 +34,7 @@
     master_hbm, first_hbm, second_hbm, grad_hbm,
     new_master, new_first, new_second, weights, rms,
     master, first, second, grad, part, parts,
-    load_sem, part_send, part_recv, line_send, line_recv, pair_send, pair_recv,
+    load_sem, part_send, part_recv, line_send, pass_send, line_recv, pair_send, pair_recv,
 ):
     my_section = lax.axis_index("section")
     my_shard = lax.axis_index("fsdp")
@@ -130,10 +130,10 @@
             device_id_type=MESH,
         )
 
-    def along(block_chip, piece, target):
+    def along(block_chip, piece, target, sends):
         block = block_chip * cores + core
         return copy(
-            block, piece, target * cores + core, line_send.at[target], line_recv.at[block_chip, piece]
+            block, piece, target * cores + core, sends.at[target], line_recv.at[block_chip, piece]
         )
 
     def over(block_chip, lane, piece):
@@ -144,34 +144,50 @@
         if cores == 2:
             over(block_chip, core, piece).start()
 
+    half = chips // 2
+    above_mid = jnp.logical_and(chip == half, core == cores - 1)
+    below_mid = jnp.logical_and(chip == half - 1, core == cores - 1)
+
+    def direct(target):
+        return jnp.logical_not(jnp.logical_and(above_mid, target < half - 1))
+
     def send(i):
         far = chips - 1 - i
         for piece in range(pieces):
 
-            @pl.when(chip + far < chips)
-            def _():
-                along(chip, piece, chip + far).start()
-
-            @pl.when(chip - far >= 0)
-            def _():
-                along(chip, piece, chip - far).start()
+            @pl.when(jnp.logical_and(chip + far < chips, direct(chip + far)))
+            def _():
+                along(chip, piece, chip + far, line_send).start()
+
+            @pl.when(jnp.logical_and(chip - far >= 0, direct(chip - far)))
+            def _():
+                along(chip, piece, chip - far, line_send).start()
 
     for_each(chips - 1, send)
     for piece in range(pieces):
         hand(chip, piece)
 
+    for piece in range(pieces):
+
+        @pl.when(below_mid)
+        def _():
+            along(half, piece, chip, line_send).wait_recv()
+            for_each(half - 1, lambda j: along(half, piece, j, pass_send).start())
+            hand(half, piece)
+
     def receive(i):
         for piece in range(pieces):
-
-            @pl.when(chip - i - 1 >= 0)
-            def _():
-                along(chip - i - 1, piece, chip).wait_recv()
-                hand(chip - i - 1, piece)
-
-            @pl.when(chip + i + 1 < chips)
-            def _():
-                along(chip + i + 1, piece, chip).wait_recv()
-                hand(chip + i + 1, piece)
+            below, above = chip - i - 1, chip + i + 1
+
+            @pl.when(below >= 0)
+            def _():
+                along(below, piece, chip, line_send).wait_recv()
+                hand(below, piece)
+
+            @pl.when(jnp.logical_and(above < chips, jnp.logical_not(jnp.logical_and(below_mid, i == 0))))
+            def _():
+                along(above, piece, chip, line_send).wait_recv()
+                hand(above, piece)
 
     for_each(chips - 1, receive)
 
@@ -184,9 +200,13 @@
             whole(i * cores + pair, pair_recv.at[i]).wait()
             whole(i * cores + core, pair_send.at[i]).wait()
 
-        @pl.when(i != chip)
+        @pl.when(jnp.logical_and(i != chip, direct(i)))
         def _():
             whole(my_shard, line_send.at[i]).wait()
+
+        @pl.when(jnp.logical_and(below_mid, i < half - 1))
+        def _():
+            whole(my_shard, pass_send.at[i]).wait()
 
     for_each(chips, finish)
     pltpu.make_async_copy(others, others, part_send).wait()
@@ -229,6 +249,7 @@
             pltpu.SemaphoreType.DMA,
             pltpu.SemaphoreType.DMA,
             pltpu.SemaphoreType.DMA((chips,)),
+            pltpu.SemaphoreType.DMA((chips,)),
             pltpu.SemaphoreType.DMA((chips, pieces)),
             pltpu.SemaphoreType.DMA((chips,)),
             pltpu.SemaphoreType.DMA((chips,)),

time: 20.6 us -> 19.8 us (0.961)
  Pallas kernels: 19.8 us -> 19 us
    pallas_call x1, Pallas kernels: 18.8 us -> 18 us  [local(): pl.pallas_call(functools.partial(step_kernel, sections, shards, params, p...]
where the time goes in v5:
time: 19.8 us; the launch traced here: 19.7 us
  Pallas kernels  19 us (96%)
  between operations  0.64 us (3%)
    pallas_call x1, Pallas kernels, local(): pl.pallas_call(functools.partial(step_kernel, sections, shards, params, p...  18 us
    pallas_call x1, Pallas kernels, local(): pl.pallas_call(store_kernel, out_shape=tuple((jax.ShapeDtypeStruct(shape,...  0.97 us

profile of v5, /device:TPU:0, one launch (start us, length us, event | category | flops | bytes accessed | tf_op | source)
XLA Modules:
  0.0 19.7 jit_solution(11068125074268286593)
XLA Ops:
  0.6 18.0 %shard_map.83 = (f32[1,8,4096]{2,1,0:T(8,128)S(1)}, f32[1,8,4096]{2,1,0:T(8,128)S(1)}, f32[1,8,4096]{2,1,0:T(8,128)S(1)}, bf16[8,8,4096]{2,1,0:T(8,128)(2,1)S(1)}, f32[8,128]{1,0:T(8,128)S(1)}) custom-call(f32[1,8,4096]{2,1,0:T(8,128)} %master_hbm.1, f32[1,8,4096]{2,1,0:T(8,128)} %first_hbm.1, f32[1,8,4096]{2,1,0:T(8,128)} %second_hbm.1, f32[1,8,4096]{2,1,0:T(8,128)} %grad_hbm.1), custom_call_target="tpu_custom_call" | custom-call | tf_op jit(solution)/shard_map/pallas_call | solution.py:239
  18.7 1.0 %shard_map.84 = (f32[1,8,4096]{2,1,0:T(8,128)}, f32[1,8,4096]{2,1,0:T(8,128)}, f32[1,8,4096]{2,1,0:T(8,128)}, bf16[8,8,4096]{2,1,0:T(8,128)(2,1)}, f32[1,1]{1,0:T(1,128)}) custom-call(f32[1,8,4096]{2,1,0:T(8,128)S(1)} %get-tuple-element.15.refs_0_, f32[1,8,4096]{2,1,0:T(8,128)S(1)} %get-tuple-element.16.refs_1_, ...), custom_call_target="tpu_custom_call" | custom-call | tf_op jit(solution)/shard_map/pallas_call | solution.py:261

commit v6 on v5

--- a/solution.py
+++ b/solution.py
@@ -16,7 +16,7 @@
 BIAS_STEPS = 10.0
 MESH = pl.DeviceIdType.MESH
 UNROLL_MOST = 40
-PIECES = 1
+PIECES = 2
 VMEM_MOST = 67043328
 GRANT_MOST = 60 * 1024 * 1024
 
@@ -34,7 +34,7 @@
     master_hbm, first_hbm, second_hbm, grad_hbm,
     new_master, new_first, new_second, weights, rms,
     master, first, second, grad, part, parts,
-    load_sem, part_send, part_recv, line_send, pass_send, line_recv, pair_send, pair_recv,
+    load_sem, part_send, part_recv, line_send, pass_send, next_send, line_recv, pair_send, pair_recv,
 ):
     my_section = lax.axis_index("section")
     my_shard = lax.axis_index("fsdp")
@@ -50,8 +50,11 @@
     loads[0].start()
 
     def peer(i):
-        s = lax.rem(my_section + i // shards, sections)
-        f = lax.rem(my_shard + i % shards, shards)
+        i = i - 1
+        step = i // sections
+        turn = shards // 2 + (step + 1) // 2 * (1 - 2 * (step % 2))
+        s = lax.rem(my_section + sections - 1 - i % sections, sections)
+        f = lax.rem(my_shard + turn + shards, shards)
         return s, f
 
     barrier = pltpu.get_barrier_semaphore()
@@ -145,11 +148,17 @@
             over(block_chip, core, piece).start()
 
     half = chips // 2
+    right_source = jnp.logical_and(chip == half - 2, core == cores - 1)
+    left_source = jnp.logical_and(
+        jnp.logical_or(chip == half, chip == half + 1), core == cores - 1
+    )
     above_mid = jnp.logical_and(chip == half, core == cores - 1)
     below_mid = jnp.logical_and(chip == half - 1, core == cores - 1)
 
     def direct(target):
-        return jnp.logical_not(jnp.logical_and(above_mid, target < half - 1))
+        right = jnp.logical_and(right_source, target > half)
+        left = jnp.logical_and(left_source, target < half - 1)
+        return jnp.logical_not(jnp.logical_or(right, left))
 
     def send(i):
         far = chips - 1 - i
@@ -169,22 +178,34 @@
 
     for piece in range(pieces):
 
+        @pl.when(above_mid)
+        def _():
+            if half > 1:
+                along(half - 2, piece, chip, line_send).wait_recv()
+                for_each(
+                    chips - 1 - half,
+                    lambda j: along(half - 2, piece, chips - 1 - j, pass_send).start(),
+                )
+                hand(half - 2, piece)
+
         @pl.when(below_mid)
         def _():
-            along(half, piece, chip, line_send).wait_recv()
-            for_each(half - 1, lambda j: along(half, piece, j, pass_send).start())
-            hand(half, piece)
+            for source, sends in ((half, pass_send), (half + 1, next_send)):
+                if source < chips:
+                    along(source, piece, chip, line_send).wait_recv()
+                    for_each(half - 1, lambda j: along(source, piece, j, sends).start())
+                    hand(source, piece)
 
     def receive(i):
         for piece in range(pieces):
             below, above = chip - i - 1, chip + i + 1
 
-            @pl.when(below >= 0)
+            @pl.when(jnp.logical_and(below >= 0, jnp.logical_not(jnp.logical_and(above_mid, i == 1))))
             def _():
                 along(below, piece, chip, line_send).wait_recv()
                 hand(below, piece)
 
-            @pl.when(jnp.logical_and(above < chips, jnp.logical_not(jnp.logical_and(below_mid, i == 0))))
+            @pl.when(jnp.logical_and(above < chips, jnp.logical_not(jnp.logical_and(below_mid, i < 2))))
             def _():
                 along(above, piece, chip, line_send).wait_recv()
                 hand(above, piece)
@@ -204,9 +225,15 @@
         def _():
             whole(my_shard, line_send.at[i]).wait()
 
-        @pl.when(jnp.logical_and(below_mid, i < half - 1))
+        @pl.when(jnp.logical_or(jnp.logical_and(above_mid, jnp.logical_and(i > half, half > 1)), jnp.logical_and(below_mid, i < half - 1)))
         def _():
             whole(my_shard, pass_send.at[i]).wait()
+
+        if half + 1 < chips:
+
+            @pl.when(jnp.logical_and(below_mid, i < half - 1))
+            def _():
+                whole(my_shard, next_send.at[i]).wait()
 
     for_each(chips, finish)
     pltpu.make_async_copy(others, others, part_send).wait()
@@ -250,6 +277,7 @@
             pltpu.SemaphoreType.DMA,
             pltpu.SemaphoreType.DMA((chips,)),
             pltpu.SemaphoreType.DMA((chips,)),
+            pltpu.SemaphoreType.DMA((chips,)),
             pltpu.SemaphoreType.DMA((chips, pieces)),
             pltpu.SemaphoreType.DMA((chips,)),
             pltpu.SemaphoreType.DMA((chips,)),

time: 19.8 us -> 19.3 us (0.975)
  Pallas kernels: 19 us -> 18.6 us
    pallas_call x1, Pallas kernels: 18 us -> 17.6 us  [local(): pl.pallas_call(functools.partial(step_kernel, sections, shards, params, p...]
where the time goes in v6:
time: 19.3 us; the launch traced here: 19.2 us
  Pallas kernels  18.6 us (96%)
  between operations  0.64 us (3%)
    pallas_call x1, Pallas kernels, local(): pl.pallas_call(functools.partial(step_kernel, sections, shards, params, p...  17.6 us
    pallas_call x1, Pallas kernels, local(): pl.pallas_call(store_kernel, out_shape=tuple((jax.ShapeDtypeStruct(shape,...  0.97 us

profile of v6, /device:TPU:0, one launch (start us, length us, event | category | flops | bytes accessed | tf_op | source)
XLA Modules:
  0.0 19.2 jit_solution(1400448764610050192)
XLA Ops:
  0.6 17.6 %shard_map.83 = (f32[1,8,4096]{2,1,0:T(8,128)S(1)}, f32[1,8,4096]{2,1,0:T(8,128)S(1)}, f32[1,8,4096]{2,1,0:T(8,128)S(1)}, bf16[8,8,4096]{2,1,0:T(8,128)(2,1)S(1)}, f32[8,128]{1,0:T(8,128)S(1)}) custom-call(f32[1,8,4096]{2,1,0:T(8,128)} %master_hbm.1, f32[1,8,4096]{2,1,0:T(8,128)} %first_hbm.1, f32[1,8,4096]{2,1,0:T(8,128)} %second_hbm.1, f32[1,8,4096]{2,1,0:T(8,128)} %grad_hbm.1), custom_call_target="tpu_custom_call" | custom-call | tf_op jit(solution)/shard_map/pallas_call | solution.py:266
  18.2 1.0 %shard_map.84 = (f32[1,8,4096]{2,1,0:T(8,128)}, f32[1,8,4096]{2,1,0:T(8,128)}, f32[1,8,4096]{2,1,0:T(8,128)}, bf16[8,8,4096]{2,1,0:T(8,128)(2,1)}, f32[1,1]{1,0:T(1,128)}) custom-call(f32[1,8,4096]{2,1,0:T(8,128)S(1)} %get-tuple-element.15.refs_0_, f32[1,8,4096]{2,1,0:T(8,128)S(1)} %get-tuple-element.16.refs_1_, ...), custom_call_target="tpu_custom_call" | custom-call | tf_op jit(solution)/shard_map/pallas_call | solution.py:289

commit v7 on v6

--- a/solution.py
+++ b/solution.py
@@ -111,10 +111,6 @@
     update = first_hat / (jnp.sqrt(second_hat) + EPSILON)
     nm = master[...] * (1.0 - LEARN_RATE * DECAY) - LEARN_RATE * update
     weights[my_shard] = nm.astype(jnp.bfloat16)
-    new_master[0] = nm
-    new_first[0] = nf
-    new_second[0] = ns
-
     cores = 2 if shards % 2 == 0 else 1
     chips = shards // cores
     core = my_shard % cores
@@ -176,6 +172,10 @@
     for piece in range(pieces):
         hand(chip, piece)
 
+    new_master[0] = nm
+    new_first[0] = nf
+    new_second[0] = ns
+
     for piece in range(pieces):
 
         @pl.when(above_mid)
@@ -197,6 +197,7 @@
                     hand(source, piece)
 
     def receive(i):
+        i = jnp.where(core == cores - 1, i, chips - 2 - i)
         for piece in range(pieces):
             below, above = chip - i - 1, chip + i + 1
 

time: 19.3 us -> 19.3 us (level)
  no operation moved by 1% of the time
where the time goes in v7:
time: 19.3 us; the launch traced here: 19.2 us
  Pallas kernels  18.6 us (96%)
  between operations  0.64 us (3%)
    pallas_call x1, Pallas kernels, local(): pl.pallas_call(functools.partial(step_kernel, sections, shards, params, p...  17.6 us
    pallas_call x1, Pallas kernels, local(): pl.pallas_call(store_kernel, out_shape=tuple((jax.ShapeDtypeStruct(shape,...  0.97 us

profile of v7, /device:TPU:0, one launch (start us, length us, event | category | flops | bytes accessed | tf_op | source)
XLA Modules:
  0.0 19.2 jit_solution(6103108347511107542)
XLA Ops:
  0.6 17.6 %shard_map.83 = (f32[1,8,4096]{2,1,0:T(8,128)S(1)}, f32[1,8,4096]{2,1,0:T(8,128)S(1)}, f32[1,8,4096]{2,1,0:T(8,128)S(1)}, bf16[8,8,4096]{2,1,0:T(8,128)(2,1)S(1)}, f32[8,128]{1,0:T(8,128)S(1)}) custom-call(f32[1,8,4096]{2,1,0:T(8,128)} %master_hbm.1, f32[1,8,4096]{2,1,0:T(8,128)} %first_hbm.1, f32[1,8,4096]{2,1,0:T(8,128)} %second_hbm.1, f32[1,8,4096]{2,1,0:T(8,128)} %grad_hbm.1), custom_call_target="tpu_custom_call" | custom-call | tf_op jit(solution)/shard_map/pallas_call | solution.py:267
  18.2 1.0 %shard_map.84 = (f32[1,8,4096]{2,1,0:T(8,128)}, f32[1,8,4096]{2,1,0:T(8,128)}, f32[1,8,4096]{2,1,0:T(8,128)}, bf16[8,8,4096]{2,1,0:T(8,128)(2,1)}, f32[1,1]{1,0:T(1,128)}) custom-call(f32[1,8,4096]{2,1,0:T(8,128)S(1)} %get-tuple-element.15.refs_0_, f32[1,8,4096]{2,1,0:T(8,128)S(1)} %get-tuple-element.16.refs_1_, ...), custom_call_target="tpu_custom_call" | custom-call | tf_op jit(solution)/shard_map/pallas_call | solution.py:290
